TPU v7x, 32 devices: a whole 2x2x4 slice. The times are simulated.
32 devices in a mesh: blk: 16 (over z, y, core), grp: 2 (over x).
Axes of the slice: x: 2, y: 2, z: 4, core: 2. Of those that a mesh axis runs over, the one named last changes fastest.
Arguments:
- layer_one: bfloat16 [1792, 1024], P(('blk', 'grp')), may hold values from -6 to 6
- layer_two: bfloat16 [1792, 1024], P(('blk', 'grp')), may hold values from -6 to 6
- spread: int32 [2], replicated, may hold values from 1024 to 4096
Outputs:
- profiles: float32 [2, 1792], P(None, ('blk', 'grp'))
- alignment: float32 [], replicated
All inputs are finite; a program needn't handle non-finite values.
Results may differ from a plain program's by a relative error of at most 0.0003.
Values may be sent and summed in bfloat16 or wider, within the bound.
A program may use at most 128 MiB of HBM per device.

v0:
```python
import jax
import jax.numpy as jnp
from jax import lax
from jax.sharding import PartitionSpec as P

D = 1024


def kernel_block(rows, sq_rows, cols, scale, offset):
    sq_cols = jnp.sum(cols.astype(jnp.float32) ** 2, axis=1)
    inner = lax.dot_general(
        rows, cols, (((1,), (1,)), ((), ())), preferred_element_type=jnp.float32
    )
    dist = sq_rows[:, None] + sq_cols[None, :] - 2.0 * inner
    return jnp.exp(-dist / (2.0 * scale)) - offset


def shards(layer_one, layer_two, spread):
    scales = spread.astype(jnp.float32)
    offsets = jnp.exp(-D / scales)
    stacked = jnp.stack([layer_one, layer_two])
    paired = lax.all_gather(stacked, "grp", axis=1, tiled=True)
    sq_pair = jnp.sum(paired.astype(jnp.float32) ** 2, axis=2)
    block = lax.all_gather(stacked, "blk", axis=1, tiled=True)
    first = kernel_block(paired[0], sq_pair[0], block[0], scales[0], offsets[0])
    second = kernel_block(paired[1], sq_pair[1], block[1], scales[1], offsets[1])
    first, second = (first, second)
    rows_acc = jnp.stack([jnp.sum(first, axis=1), jnp.sum(second, axis=1)])
    prods = jnp.stack([jnp.sum(first * second), jnp.sum(first * first), jnp.sum(second * second)])
    rows_acc, prods = (rows_acc, prods)
    own_rows = lax.psum_scatter(rows_acc, "grp", scatter_dimension=1, tiled=True)
    total = own_rows.shape[1] * lax.axis_size("blk") * lax.axis_size("grp")
    row_terms = jnp.stack(
        [
            jnp.sum(own_rows[0]),
            jnp.sum(own_rows[1]),
            jnp.sum(own_rows[0] * own_rows[1]),
            jnp.sum(own_rows[0] * own_rows[0]),
            jnp.sum(own_rows[1] * own_rows[1]),
        ]
    )
    prods = lax.psum(prods, ("blk", "grp"))
    row_terms = lax.psum(row_terms, ("blk", "grp"))
    sum_one, sum_two = (row_terms[0], row_terms[1])
    c_cross, c_one, c_two = (row_terms[2], row_terms[3], row_terms[4])
    h_cross = prods[0] - 2.0 * c_cross / total + sum_one * sum_two / (total * total)
    h_one = prods[1] - 2.0 * c_one / total + sum_one * sum_one / (total * total)
    h_two = prods[2] - 2.0 * c_two / total + sum_two * sum_two / (total * total)
    alignment = h_cross / jnp.sqrt(h_one * h_two)
    profiles = jnp.stack(
        [own_rows[0] / jnp.sqrt(c_one / total), own_rows[1] / jnp.sqrt(c_two / total)]
    )
    return (profiles, alignment)


def solution(mesh):
    return jax.shard_map(
        shards,
        mesh=mesh,
        in_specs=(P(("blk", "grp"), None), P(("blk", "grp"), None), P()),
        out_specs=(P(None, ("blk", "grp")), P()),
        check_vma=False,
    )
```

profile of v0, /device:TPU:0, one launch (start us, length us, event | category | flops | bytes accessed | tf_op | source)
XLA Modules:
  0.0 135.6 jit_solution(13423032327136159622)
XLA Ops:
  7.2 0.0 all-gather.2.cloned.1.call-start
  7.2 1.7 %pad_maximum_fusion = bf16[2,56,1024]{2,1,0:T(8,128)(2,1)} fusion(bf16[1,56,1024]{2,1,0:T(8,128)(2,1)} %bitcast.70, bf16[1,56,1024]{2,1,0:T(8,128)(2,1)} %bitcast.71), kind=kLoop, calls=%fused_computation.24 | loop fusion | flops 114688 | bytes 458752 | tf_op jit(solution)/shard_map/stack | solution.py:21
  8.9 0.0 all-gather.2.cloned.1.call-update
  8.9 0.7 convert_element_type.14
  9.6 0.6 fusion.16
  11.5 1.2 dynamic-slice
  13.4 0.7 divide_exponential_fusion
  14.0 0.6 fusion.17
  14.6 9.5 %all_gather.6 = bf16[2,112,1024]{2,1,0:T(8,128)(2,1)S(1)} all-gather(bf16[2,56,1024]{2,1,0:T(8,128)(2,1)} %pad_maximum_fusion), channel_id=1, replica_groups=mesh['blk'=16,'grp'=2] {'grp'}, dimensions={1}, use_global_device_ids=true | all-gather | bytes 688128 | tf_op jit(solution)/shard_map/all_gather | solution.py:22
  24.1 0.2 multiply_reduce_fusion.2
  24.3 36.4 %all-gather.2.cloned.1.call-done = bf16[2,896,1024]{2,1,0:T(8,128)(2,1)} async-done(((bf16[2,56,1024]{2,1,0:T(8,128)(2,1)}), bf16[2,896,1024]{2,1,0:T(8,128)(2,1)}) %all-gather.2.cloned.1.call-update) | async-done | bytes 3670032 | tf_op jit(solution)/shard_map/all_gather | solution.py:24
  60.7 0.0 copy-start
  60.7 3.0 %multiply_reduce_fusion.1 = (f32[896]{0:T(1024)S(1)}, f32[896]{0:T(1024)S(1)}) fusion(bf16[2,896,1024]{2,1,0:T(8,128)(2,1)} %all-gather.2.cloned.1.call-done), kind=kLoop, calls=%fused_computation.1 | loop fusion | flops 5503232 | bytes 3677184 | tf_op jit(solution)/shard_map/reduce_sum | solution.py:10
  63.7 0.2 copy-done
  63.8 1.4 %fusion.10 = f32[112,896]{1,0:T(8,128)S(1)} fusion(bf16[2,896,1024]{2,1,0:T(8,128)(2,1)S(1)} %copy-done, bf16[2,112,1024]{2,1,0:T(8,128)(2,1)S(1)} %all_gather.6, f32[]{:T(128)} %bitcast.12, f32[]{:T(128)} %bitcast.11, f32[896]{0:T(1024)S(1)} %get-tuple-element.3, f32[112]{0:T(128)S(1)} %get-tuple-element.18), kind=kOutput, calls=%fused_computation.14 | convolution fusion | flops 206123008 | bytes 2470408 | tf_op jit(solution)/shard_map/dot_general | solution.py:11
  65.2 2.1 %multiply_reduce_fusion.5 = (f32[]{:T(128)}, f32[]{:T(128)}, f32[112]{0:T(128)S(1)}, f32[]{:T(128)}, f32[112]{0:T(128)S(1)}) fusion(f32[112,896]{1,0:T(8,128)S(1)} %fusion.10, f32[]{:T(128)} %bitcast.6, f32[]{:T(128)} %bitcast.5, bf16[2,896,1024]{2,1,0:T(8,128)(2,1)S(1)} %copy-done, bf16[2,112,1024]{2,1,0:T(8,128)(2,1)S(1)} %all_gather.6, ...), kind=kOutput, calls=%fused_computation.21 | convolution fusion | flops 206925600 | bytes 2471316 | tf_op jit(solution)/shard_map/dot_general | solution.py:11
  67.4 4.9 %all-reduce = f32[2,112]{1,0:T(2,128)S(1)} all-reduce(f32[2,112]{1,0:T(2,128)S(1)} %pad_maximum_fusion.1), channel_id=2, replica_groups=mesh['blk'=16,'grp'=2] {'grp'}, use_global_device_ids=true, to_apply=%region_5.0.clone | all-reduce | flops 224 | bytes 1792
  72.3 0.1 constant_dynamic-slice_fusion
  72.4 0.7 multiply_reduce_fusion.6
  73.0 2.0 %pad_maximum_fusion.3 = f32[3]{0:T(128)S(1)} fusion(f32[1]{0:T(128)} %bitcast.23, f32[1]{0:T(128)} %bitcast.22, f32[1]{0:T(128)} %bitcast.21), kind=kLoop, calls=%fused_computation.27 | loop fusion | flops 6 | bytes 24 | tf_op jit(solution)/shard_map/stack | solution.py:29
  75.0 3.2 %stack.64 = f32[5]{0:T(128)S(1)} concatenate(f32[1]{0:T(128)} %bitcast.14, f32[1]{0:T(128)} %bitcast.15, f32[1]{0:T(128)} %bitcast.16, f32[1]{0:T(128)} %bitcast.17, f32[1]{0:T(128)} %bitcast.18), dimensions={0} | concatenate | bytes 40 | tf_op jit(solution)/shard_map/stack | solution.py:33
  78.2 39.4 %all-reduce.1 = (f32[5]{0:T(128)S(1)}, f32[3]{0:T(128)S(1)}) all-reduce(f32[5]{0:T(128)S(1)} %stack.64, f32[3]{0:T(128)S(1)} %pad_maximum_fusion.3), channel_id=1, replica_groups=mesh['blk'=16,'grp'=2] {'blk','grp'}, use_global_device_ids=true, to_apply=%region_11.0 | all-reduce | flops 8 | bytes 64 | tf_op jit(solution)/shard_map/psum | solution.py:43
  117.6 0.7 fusion.14
  127.1 0.6 pad_maximum_fusion.2
  (3 shorter events, 0.0 us)
Async XLA Ops:
  7.2 53.5 %all-gather.2.cloned.1.call-start = ((), (), s32[]{:S(2)}) async-start(), calls=%async_computation | async-start | bytes 3899392 | tf_op jit(solution)/shard_map/all_gather | solution.py:24
  60.7 3.1 %copy-start = (bf16[2,896,1024]{2,1,0:T(8,128)(2,1)S(1)}, bf16[2,896,1024]{2,1,0:T(8,128)(2,1)}, u32[]{:S(2)}) copy-start(bf16[2,896,1024]{2,1,0:T(8,128)(2,1)} %all-gather.2.cloned.1.call-done) | copy-start | bytes 11010052
Sparse Core Ops, SparseCore 0:
  10.3 50.3 all-gather.1
where the time goes:
time: 136 us
  blocking collectives  53.8 us (40%)
  waiting for transfers between devices  36.4 us (27%)
  between operations  26 us (19%)
  other arithmetic  9.38 us (7%)
  local copies, waits for them, and re-layouts  6.55 us (5%)
  matrix products  3.5 us (3%)
    psum x1, blocking collectives, shards(): row_terms = lax.psum(row_terms, ('blk', 'grp'))  39.4 us
    all_gather x1, waiting for transfers between devices, shards(): block = lax.all_gather(stacked, 'blk', axis=1, tiled=True)  36.4 us
    all_gather x1, blocking collectives, shards(): paired = lax.all_gather(stacked, 'grp', axis=1, tiled=True)  9.49 us
    unnamed x1, blocking collectives  4.91 us
    dot_general x2, matrix products, kernel_block(): lax.dot_general(rows, cols, (((1,), (1,)), ((), ())), preferred_element_t...  3.5 us
    another operation x1, local copies, waits for them, and re-layouts, shards(): jnp.stack([jnp.sum(own_rows[0]), jnp.sum(own_rows[1]), jnp.sum(own_rows[0...  3.22 us
    reduce_sum x1, other arithmetic, kernel_block(): sq_cols = jnp.sum(cols.astype(jnp.float32) ** 2, axis=1)  2.99 us
  transfers between devices with their start and end apart: 1, of which 1 were waited for; matrix products, arithmetic and copies ran while one was open for 3% of the time, Pallas kernels for 0%

commit v1 on v0

v1 whole, which is shorter than its diff:
```python
import functools

import jax
import jax.numpy as jnp
from jax import lax
from jax.experimental import pallas as pl
from jax.experimental.pallas import tpu as pltpu
from jax.sharding import PartitionSpec as P

MESH = pl.DeviceIdType.MESH
LANES = 128
PLANE = 4


def reach(planes, src):
    if planes % 2:
        return planes // 2
    ahead = 1 - (2 * src) // planes
    odd = (src - (planes // 2) * (1 - ahead)) % 2
    return planes // 2 - 1 + ahead * (1 - odd) + (1 - ahead) * odd


def round_up(value, step):
    return -(-value // step) * step


def body(blks, grps, rows, one_ref, two_ref, spread_ref, prof_ref, align_ref, plane, column, outbox, inbox, col_out, col_in, sums, got,
         load_sem, psend, precv, csend, crecv, osend, orecv, rsend, rrecv, ssend, srecv):
    planes = blks // PLANE
    n = blks * grps
    depth = one_ref.shape[1]
    pad = plane.shape[2] // (2 * 4)
    width = plane.shape[2]
    half = depth // 2
    blk = lax.axis_index("blk")
    grp = lax.axis_index("grp")
    k = blk // PLANE
    y = (blk // 2) % 2
    core = blk % 2
    me = blk * grps + grp

    def at(plane_at, y_at, core_at, grp_at):
        return (plane_at * PLANE + y_at * 2 + core_at, grp_at)

    def place(slot, side):
        return (slot * 2 + side) * pad

    loads = []
    for layer, ref in enumerate((one_ref, two_ref)):
        copy = pltpu.make_async_copy(ref, plane.at[layer, 0, pl.ds(0, rows)], load_sem.at[layer])
        copy.start()
        loads.append(copy)

    barrier = pltpu.get_barrier_semaphore()

    def greet(off, carry):
        other = lax.rem(me + off, n)
        pl.semaphore_signal(barrier, inc=1, device_id=(other // grps, other % grps), device_id_type=MESH)
        return carry

    lax.fori_loop(1, n, greet, 0)
    for copy in loads:
        copy.wait()
    pl.semaphore_wait(barrier, n - 1)

    x_peer = at(k, y, core, 1 - grp)
    y_peer = at(k, 1 - y, core, grp)
    d_peer = at(k, 1 - y, core, 1 - grp)
    peers = (None, x_peer, y_peer, d_peer)
    mates = (at(k, y, 1 - core, grp), at(k, y, 1 - core, 1 - grp), at(k, 1 - y, 1 - core, grp), at(k, 1 - y, 1 - core, 1 - grp))

    def plane_copy(layer, src, slot, side, device):
        return pltpu.make_async_remote_copy(
            src_ref=plane.at[layer, 0, pl.ds(place(*src), rows)],
            dst_ref=plane.at[layer, 0, pl.ds(place(slot, side), rows)],
            send_sem=psend.at[slot, side, layer],
            recv_sem=precv.at[slot, side, layer],
            device_id=device,
            device_id_type=MESH,
        )

    def x_own(layer):
        return plane_copy(layer, (0, 0), 1, 0, x_peer)

    def y_own(layer):
        return plane_copy(layer, (0, 0), 2, 0, y_peer)

    def diag(layer):
        if layer == 0:
            return plane_copy(0, (1, 0), 3, 0, y_peer)
        return plane_copy(1, (2, 0), 3, 0, x_peer)

    def mate(slot, layer):
        return plane_copy(layer, (slot, 0), slot, 1, mates[0])

    def col_copy(src, way, layer, part, own, dst):
        if own:
            ref = plane.at[layer, 0, pl.ds(0, rows), pl.ds(part * half, half)]
        else:
            ref = column.at[src, layer, pl.ds(0, rows), pl.ds(part * half, half)]
        return pltpu.make_async_remote_copy(
            src_ref=ref,
            dst_ref=column.at[src, layer, pl.ds(0, rows), pl.ds(part * half, half)],
            send_sem=csend.at[src, way, layer, part],
            recv_sem=crecv.at[src, layer, part],
            device_id=at(dst, y, core, grp),
            device_id_type=MESH,
        )

    pieces = [(layer, part) for layer in range(2) for part in range(2)]

    def gets(src, dst):
        gap = (dst - src + 2 * planes) % planes
        return (src >= 0) & (src < planes) & (dst >= 0) & (dst < planes) & (gap > 0) & (gap <= reach(planes, src))

    last_down = k + reach(planes, k) - planes
    starts = ((0, k + 1, gets(k, k + 1)), (1, last_down, last_down >= 0))

    def each_source(work):
        def step(index, carry):
            way = index % 2
            src = k - (index // 2 + 1) * (1 - 2 * way)
            onward = k + 1 - 2 * way

            @pl.when(gets(src, k))
            def _():
                work(src, way, onward, gets(src, onward) & (onward != src))

            return carry

        lax.fori_loop(0, 2 * (planes - 1), step, 0)

    x_own(0).start()
    y_own(1).start()
    for way, dst, goes in starts:
        @pl.when(goes)
        def _(way=way, dst=dst):
            for layer, part in pieces:
                col_copy(k, way, layer, part, True, dst).start()
    x_own(1).start()
    y_own(0).start()
    mate(0, 0).start()
    mate(0, 1).start()

    def relay(layer):
        def work(src, way, onward, goes):
            @pl.when(goes)
            def _():
                for part in range(2):
                    col_copy(src, way, layer, part, False, onward).wait_recv()
                    col_copy(src, way, layer, part, False, onward).start()

        each_source(work)

    x_own(0).wait_recv()
    diag(0).start()
    mate(1, 0).start()
    y_own(1).wait_recv()
    diag(1).start()
    mate(2, 1).start()
    relay(0)
    x_own(1).wait_recv()
    mate(1, 1).start()
    y_own(0).wait_recv()
    mate(2, 0).start()
    relay(1)
    for layer in range(2):
        diag(layer).wait_recv()
        mate(3, layer).start()
    for slot in range(4):
        for layer in range(2):
            mate(slot, layer).wait_recv()

    scales = [jnp.full((1, 1), spread_ref[layer], jnp.int32).astype(jnp.float32) for layer in range(2)]
    rates = [-0.5 / scale for scale in scales]
    offsets = [jnp.exp(-depth / scale) for scale in scales]
    row_ok = lax.broadcasted_iota(jnp.int32, (pad, width), 0) < rows
    col_ok = lax.broadcasted_iota(jnp.int32, (pad, width), 1) % pad < rows
    ok = row_ok & col_ok

    def squares(block):
        wide = block.astype(jnp.float32)
        return jnp.sum(wide * wide, axis=1, keepdims=True)

    sq_cols = []
    for layer in range(2):
        parts = []
        for piece in range(width // LANES):
            sq = squares(plane[layer, 0, piece * LANES:(piece + 1) * LANES, :])
            parts.append(jnp.transpose(jnp.broadcast_to(sq, (LANES, LANES)))[0:1, :])
        sq_cols.append(jnp.concatenate(parts, axis=1))

    def kernel_block(layer, block):
        inner = lax.dot_general(block, plane[layer, 0], (((1,), (1,)), ((), ())), preferred_element_type=jnp.float32)
        dist = squares(block) + sq_cols[layer] - 2.0 * inner
        return jnp.where(ok, jnp.exp(dist * rates[layer]) - offsets[layer], 0.0)

    def fold(value):
        total = value[:, 0:LANES]
        for piece in range(1, width // LANES):
            total = total + value[:, piece * LANES:(piece + 1) * LANES]
        return total

    def row_sums(value):
        part = fold(value)
        if pad < LANES:
            part = jnp.concatenate([part, jnp.zeros((LANES - pad, LANES), jnp.float32)], axis=0)
        return jnp.sum(jnp.transpose(part), axis=0, keepdims=True)

    def lane_sums(value):
        return jnp.sum(fold(value), axis=0, keepdims=True)

    own = [kernel_block(layer, plane[layer, 0, 0:pad, :]) for layer in range(2)]
    sums[0:1, :] = row_sums(own[0])
    sums[1:2, :] = row_sums(own[1])
    sums[2:3, :] = lane_sums(own[0] * own[1])
    sums[3:4, :] = lane_sums(own[0] * own[0])
    sums[4:5, :] = lane_sums(own[1] * own[1])
    outbox[...] = jnp.zeros_like(outbox)
    col_out[...] = jnp.zeros_like(col_out)

    def back(src, dst):
        return pltpu.make_async_remote_copy(
            src_ref=col_out.at[src],
            dst_ref=col_in.at[dst],
            send_sem=rsend.at[src],
            recv_sem=rrecv.at[dst],
            device_id=at(src, y, core, grp),
            device_id_type=MESH,
        )

    def meet(src, way, onward, goes):
        @pl.when(jnp.logical_not(goes))
        def _():
            for layer, part in pieces:
                col_copy(src, way, layer, part, False, k).wait_recv()

        met = [kernel_block(layer, column[src, layer]) for layer in range(2)]
        for layer in range(2):
            col_out[src, layer:layer + 1, :] = row_sums(met[layer])
        back(src, k).start()
        sums[2:3, :] += 2.0 * lane_sums(met[0] * met[1])
        sums[3:4, :] += 2.0 * lane_sums(met[0] * met[0])
        sums[4:5, :] += 2.0 * lane_sums(met[1] * met[1])
        for layer in range(2):
            across = jnp.sum(met[layer], axis=0, keepdims=True)
            for place_at in range(8):
                outbox[place_at, layer:layer + 1, 0:pad] += across[:, place_at * pad:(place_at + 1) * pad]

    each_source(meet)

    def share(place_at):
        slot, side = place_at // 2, place_at % 2
        device = mates[slot] if side else peers[slot]
        return pltpu.make_async_remote_copy(
            src_ref=outbox.at[place_at],
            dst_ref=inbox.at[place_at],
            send_sem=osend.at[place_at],
            recv_sem=orecv.at[place_at],
            device_id=device,
            device_id_type=MESH,
        )

    for place_at in range(7, 0, -1):
        share(place_at).start()
    sums[0:2, :] += outbox[0, 0:2, :]
    for place_at in range(1, 8):
        share(place_at).wait_recv()
        sums[0:2, :] += inbox[place_at, 0:2, :]
    def collect(dst, carry):
        @pl.when(gets(k, dst))
        def _():
            back(k, dst).wait_recv()
            sums[0:2, :] += col_in[dst, 0:2, :]

        return carry

    lax.fori_loop(0, planes, collect, 0)

    first, second = sums[0:1, :], sums[1:2, :]
    terms = jnp.concatenate([sums[2:5, :], first, second, first * second, first * first, second * second], axis=0)
    totals = jnp.sum(terms, axis=1, keepdims=True)
    spread_out = lax.broadcasted_iota(jnp.int32, (8, LANES), 0) == lax.broadcasted_iota(jnp.int32, (8, LANES), 1)
    got[0] = jnp.sum(jnp.where(spread_out, totals, 0.0), axis=0, keepdims=True)

    def tell(off):
        other = lax.rem(me + off, n)
        return pltpu.make_async_remote_copy(
            src_ref=got.at[0],
            dst_ref=got.at[off],
            send_sem=ssend.at[off],
            recv_sem=srecv.at[off],
            device_id=(other // grps, other % grps),
            device_id_type=MESH,
        )

    def each_other(act):
        def step(off, carry):
            act(tell(off))
            return carry

        lax.fori_loop(1, n, step, 0)

    each_other(lambda copy: copy.start())

    for layer in range(2):
        x_own(layer).wait_send()
        y_own(layer).wait_send()
        diag(layer).wait_send()
        for slot in range(4):
            mate(slot, layer).wait_send()
    for way, dst, goes in starts:
        @pl.when(goes)
        def _(way=way, dst=dst):
            for layer, part in pieces:
                col_copy(k, way, layer, part, True, dst).wait_send()

    def drain(src, way, onward, goes):
        back(src, k).wait_send()

        @pl.when(goes)
        def _():
            for layer, part in pieces:
                col_copy(src, way, layer, part, False, onward).wait_send()

    each_source(drain)
    for place_at in range(1, 8):
        share(place_at).wait_send()

    each_other(lambda copy: copy.wait_recv())
    each_other(lambda copy: copy.wait_send())
    final = jnp.sum(got[...], axis=0)
    f_cross, f_one, f_two, s_one, s_two, c_cross, c_one, c_two = (final[:, at_lane:at_lane + 1] for at_lane in range(8))
    total = float(n * rows)
    h_cross = f_cross - 2.0 * c_cross / total + s_one * s_two / (total * total)
    h_one = f_one - 2.0 * c_one / total + s_one * s_one / (total * total)
    h_two = f_two - 2.0 * c_two / total + s_two * s_two / (total * total)
    align_ref[...] = h_cross / jnp.sqrt(h_one * h_two)
    prof_ref[0:1, :] = first[:, 0:rows] / jnp.sqrt(c_one / total)
    prof_ref[1:2, :] = second[:, 0:rows] / jnp.sqrt(c_two / total)


def shards(blks, grps, layer_one, layer_two, spread):
    rows, depth = layer_one.shape
    pad = round_up(rows, 64)
    planes, n = blks // PLANE, blks * grps
    dma = pltpu.SemaphoreType.DMA
    profiles, alignment = pl.pallas_call(
        functools.partial(body, blks, grps, rows),
        out_shape=(jax.ShapeDtypeStruct((2, rows), jnp.float32), jax.ShapeDtypeStruct((1, 1), jnp.float32)),
        in_specs=[pl.BlockSpec(memory_space=pl.ANY), pl.BlockSpec(memory_space=pl.ANY), pl.BlockSpec(memory_space=pltpu.SMEM)],
        out_specs=(pl.BlockSpec(memory_space=pltpu.VMEM), pl.BlockSpec(memory_space=pltpu.VMEM)),
        scratch_shapes=[
            pltpu.VMEM((2, 1, 8 * pad, depth), jnp.bfloat16),
            pltpu.VMEM((planes, 2, pad, depth), jnp.bfloat16),
            pltpu.VMEM((8, 8, LANES), jnp.float32),
            pltpu.VMEM((8, 8, LANES), jnp.float32),
            pltpu.VMEM((planes, 8, LANES), jnp.float32),
            pltpu.VMEM((planes, 8, LANES), jnp.float32),
            pltpu.VMEM((8, LANES), jnp.float32),
            pltpu.VMEM((n, 1, LANES), jnp.float32),
            dma((2,)),
            dma((4, 2, 2)),
            dma((4, 2, 2)),
            dma((planes, 2, 2, 2)),
            dma((planes, 2, 2)),
            dma((8,)),
            dma((8,)),
            dma((planes,)),
            dma((planes,)),
            dma((n,)),
            dma((n,)),
        ],
        compiler_params=pltpu.CompilerParams(collective_id=0, has_side_effects=True),
    )(layer_one, layer_two, spread)
    return (profiles, alignment.reshape(()))


def solution(mesh):
    return jax.shard_map(
        functools.partial(shards, mesh.shape["blk"], mesh.shape["grp"]),
        mesh=mesh,
        in_specs=(P(("blk", "grp"), None), P(("blk", "grp"), None), P()),
        out_specs=(P(None, ("blk", "grp")), P()),
        check_vma=False,
    )
```

time: 136 us -> 34 us (0.25)
  blocking collectives: 53.8 us -> 0 us
  waiting for transfers between devices: 36.4 us -> 0 us
  Pallas kernels: 0 us -> 30.2 us
  between operations: 26 us -> 2.41 us
  other arithmetic: 9.38 us -> 0 us
  local copies, waits for them, and re-layouts: 6.55 us -> 1.21 us
  matrix products: 3.5 us -> 0 us
    psum x1 -> x0, blocking collectives: 39.4 us -> none  [shards(): row_terms = lax.psum(row_terms, ('blk', 'grp'))]
    all_gather x1 -> x0, waiting for transfers between devices: 36.4 us -> none  [shards(): block = lax.all_gather(stacked, 'blk', axis=1, tiled=True)]
    pallas_call x0 -> x1, Pallas kernels: none -> 30.2 us  [shards(): pl.pallas_call(functools.partial(body, blks, grps, rows), out_shape=(jax....]
    all_gather x1 -> x0, blocking collectives: 9.49 us -> none  [shards(): paired = lax.all_gather(stacked, 'grp', axis=1, tiled=True)]
    unnamed x1 -> x0, blocking collectives: 4.91 us -> none
    another operation x4 -> x0, other arithmetic: 4.21 us -> none  [the longest x1 1.97 us: shards(): jnp.stack([jnp.sum(first * second), jnp.sum(first * first), jnp.sum(secon...]
    reduce_sum x3 -> x0, other arithmetic: 3.84 us -> none  [the longest x1 2.99 us: kernel_block(): sq_cols = jnp.sum(cols.astype(jnp.float32) ** 2, axis=1)]
    dot_general x2 -> x0, matrix products: 3.5 us -> none  [kernel_block(): lax.dot_general(rows, cols, (((1,), (1,)), ((), ())), preferred_element_t...]
  transfers between devices with their start and end apart: 1 -> 0, of which waited for: 1 -> 0; matrix products, arithmetic and copies ran while one was open for 3% -> 0% of each run, Pallas kernels for 0% -> 0%
where the time goes in v1:
time: 34 us; the launch traced here: 33.9 us
  Pallas kernels  30.2 us (89%)
  between operations  2.41 us (7%)
  local copies, waits for them, and re-layouts  1.21 us (4%)
    pallas_call x1, Pallas kernels, shards(): pl.pallas_call(functools.partial(body, blks, grps, rows), out_shape=(jax....  30.2 us
    unnamed x3, local copies, waits for them, and re-layouts  1.21 us

profile of v1, /device:TPU:0, one launch (start us, length us, event | category | flops | bytes accessed | tf_op | source)
XLA Modules:
  0.0 33.9 jit_solution(13172728322677977203)
XLA Ops:
  0.6 30.2 %shard_map.50 = (f32[2,56]{1,0:T(2,128)}, f32[1,1]{1,0:T(1,128)}) custom-call(bf16[56,1024]{1,0:T(8,128)(2,1)} %one_ref.1, bf16[56,1024]{1,0:T(8,128)(2,1)} %two_ref.1, s32[2]{0:T(128)} %spread_ref.1), custom_call_target="tpu_custom_call" | custom-call | tf_op jit(solution)/shard_map/pallas_call | solution.py:348
  30.9 0.0 copy-start
  30.9 0.6 %copy-done = f32[2,56]{1,0:T(2,128)S(1)} copy-done((f32[2,56]{1,0:T(2,128)S(1)}, f32[2,56]{1,0:T(2,128)}, u32[]{:S(2)}) %copy-start) | copy-done | bytes 472
  31.5 0.6 %copy.7 = f32[2,56]{1,0:T(2,128)} copy(f32[2,56]{1,0:T(2,128)S(1)} %copy-done) | data formatting | bytes 896
Async XLA Ops:
  30.9 0.7 %copy-start = (f32[2,56]{1,0:T(2,128)S(1)}, f32[2,56]{1,0:T(2,128)}, u32[]{:S(2)}) copy-start(f32[2,56]{1,0:T(2,128)} %get-tuple-element.8) | copy-start | bytes 1348

commit v2 on v1

--- a/solution.py
+++ b/solution.py
@@ -53,18 +53,26 @@
 
     barrier = pltpu.get_barrier_semaphore()
 
-    def greet(off, carry):
-        other = lax.rem(me + off, n)
-        pl.semaphore_signal(barrier, inc=1, device_id=(other // grps, other % grps), device_id_type=MESH)
-        return carry
-
-    lax.fori_loop(1, n, greet, 0)
+    last_down = k + reach(planes, k) - planes
+    x_peer = at(k, y, core, 1 - grp)
+    y_peer = at(k, 1 - y, core, grp)
+    for device in (x_peer, y_peer, at(k, y, 1 - core, grp)):
+        pl.semaphore_signal(barrier, inc=1, device_id=device, device_id_type=MESH)
+
+    def greet(far, count):
+        linked = (far == k + 1) | (far == k - 1) | (far == last_down) | (far + reach(planes, far) - planes == k)
+
+        @pl.when(linked)
+        def _():
+            pl.semaphore_signal(barrier, inc=1, device_id=at(far, y, core, grp), device_id_type=MESH)
+
+        return count + linked.astype(jnp.int32)
+
+    partners = lax.fori_loop(0, planes, greet, jnp.int32(3))
     for copy in loads:
         copy.wait()
-    pl.semaphore_wait(barrier, n - 1)
-
-    x_peer = at(k, y, core, 1 - grp)
-    y_peer = at(k, 1 - y, core, grp)
+    pl.semaphore_wait(barrier, partners)
+
     d_peer = at(k, 1 - y, core, 1 - grp)
     peers = (None, x_peer, y_peer, d_peer)
     mates = (at(k, y, 1 - core, grp), at(k, y, 1 - core, 1 - grp), at(k, 1 - y, 1 - core, grp), at(k, 1 - y, 1 - core, 1 - grp))
@@ -113,7 +121,6 @@
         gap = (dst - src + 2 * planes) % planes
         return (src >= 0) & (src < planes) & (dst >= 0) & (dst < planes) & (gap > 0) & (gap <= reach(planes, src))
 
-    last_down = k + reach(planes, k) - planes
     starts = ((0, k + 1, gets(k, k + 1)), (1, last_down, last_down >= 0))
 
     def each_source(work):
@@ -255,8 +262,8 @@
         return pltpu.make_async_remote_copy(
             src_ref=outbox.at[place_at],
             dst_ref=inbox.at[place_at],
-            send_sem=osend.at[place_at],
-            recv_sem=orecv.at[place_at],
+            send_sem=osend.at[0],
+            recv_sem=orecv.at[0],
             device_id=device,
             device_id_type=MESH,
         )
@@ -264,9 +271,9 @@
     for place_at in range(7, 0, -1):
         share(place_at).start()
     sums[0:2, :] += outbox[0, 0:2, :]
-    for place_at in range(1, 8):
-        share(place_at).wait_recv()
-        sums[0:2, :] += inbox[place_at, 0:2, :]
+    shared = inbox.at[pl.ds(1, 7)]
+    pltpu.make_async_copy(shared, shared, orecv.at[0]).wait()
+    sums[0:2, :] += jnp.sum(inbox[1:8], axis=0)
     def collect(dst, carry):
         @pl.when(gets(k, dst))
         def _():
@@ -288,20 +295,17 @@
         return pltpu.make_async_remote_copy(
             src_ref=got.at[0],
             dst_ref=got.at[off],
-            send_sem=ssend.at[off],
-            recv_sem=srecv.at[off],
+            send_sem=ssend.at[0],
+            recv_sem=srecv.at[0],
             device_id=(other // grps, other % grps),
             device_id_type=MESH,
         )
 
-    def each_other(act):
-        def step(off, carry):
-            act(tell(off))
-            return carry
-
-        lax.fori_loop(1, n, step, 0)
-
-    each_other(lambda copy: copy.start())
+    def start_tell(off, carry):
+        tell(off).start()
+        return carry
+
+    lax.fori_loop(1, n, start_tell, 0, unroll=n <= 64)
 
     for layer in range(2):
         x_own(layer).wait_send()
@@ -324,11 +328,11 @@
                 col_copy(src, way, layer, part, False, onward).wait_send()
 
     each_source(drain)
-    for place_at in range(1, 8):
-        share(place_at).wait_send()
-
-    each_other(lambda copy: copy.wait_recv())
-    each_other(lambda copy: copy.wait_send())
+    pltpu.make_async_copy(shared, shared, osend.at[0]).wait()
+
+    all_told = got.at[pl.ds(1, n - 1)]
+    pltpu.make_async_copy(all_told, all_told, srecv.at[0]).wait()
+    pltpu.make_async_copy(all_told, all_told, ssend.at[0]).wait()
     final = jnp.sum(got[...], axis=0)
     f_cross, f_one, f_two, s_one, s_two, c_cross, c_one, c_two = (final[:, at_lane:at_lane + 1] for at_lane in range(8))
     total = float(n * rows)
@@ -353,10 +357,10 @@
         scratch_shapes=[
             pltpu.VMEM((2, 1, 8 * pad, depth), jnp.bfloat16),
             pltpu.VMEM((planes, 2, pad, depth), jnp.bfloat16),
-            pltpu.VMEM((8, 8, LANES), jnp.float32),
-            pltpu.VMEM((8, 8, LANES), jnp.float32),
-            pltpu.VMEM((planes, 8, LANES), jnp.float32),
-            pltpu.VMEM((planes, 8, LANES), jnp.float32),
+            pltpu.VMEM((8, 2, LANES), jnp.float32),
+            pltpu.VMEM((8, 2, LANES), jnp.float32),
+            pltpu.VMEM((planes, 2, LANES), jnp.float32),
+            pltpu.VMEM((planes, 2, LANES), jnp.float32),
             pltpu.VMEM((8, LANES), jnp.float32),
             pltpu.VMEM((n, 1, LANES), jnp.float32),
             dma((2,)),

time: 34 us -> 32.2 us (0.947)
  Pallas kernels: 30.2 us -> 28.4 us
    pallas_call x1, Pallas kernels: 30.2 us -> 28.4 us  [shards(): pl.pallas_call(functools.partial(body, blks, grps, rows), out_shape=(jax....]
where the time goes in v2:
time: 32.2 us; the launch traced here: 32 us
  Pallas kernels  28.4 us (88%)
  between operations  2.41 us (7%)
  local copies, waits for them, and re-layouts  1.21 us (4%)
    pallas_call x1, Pallas kernels, shards(): pl.pallas_call(functools.partial(body, blks, grps, rows), out_shape=(jax....  28.4 us
    unnamed x3, local copies, waits for them, and re-layouts  1.21 us

profile of v2, /device:TPU:0, one launch (start us, length us, event | category | flops | bytes accessed | tf_op | source)
XLA Modules:
  0.0 32.0 jit_solution(14504315716514087902)
XLA Ops:
  0.6 28.4 %shard_map.50 = (f32[2,56]{1,0:T(2,128)}, f32[1,1]{1,0:T(1,128)}) custom-call(bf16[56,1024]{1,0:T(8,128)(2,1)} %one_ref.1, bf16[56,1024]{1,0:T(8,128)(2,1)} %two_ref.1, s32[2]{0:T(128)} %spread_ref.1), custom_call_target="tpu_custom_call" | custom-call | tf_op jit(solution)/shard_map/pallas_call | solution.py:352
  29.0 0.0 copy-start
  29.0 0.6 %copy-done = f32[2,56]{1,0:T(2,128)S(1)} copy-done((f32[2,56]{1,0:T(2,128)S(1)}, f32[2,56]{1,0:T(2,128)}, u32[]{:S(2)}) %copy-start) | copy-done | bytes 472
  29.7 0.6 %copy.7 = f32[2,56]{1,0:T(2,128)} copy(f32[2,56]{1,0:T(2,128)S(1)} %copy-done) | data formatting | bytes 896
Async XLA Ops:
  29.0 0.7 %copy-start = (f32[2,56]{1,0:T(2,128)S(1)}, f32[2,56]{1,0:T(2,128)}, u32[]{:S(2)}) copy-start(f32[2,56]{1,0:T(2,128)} %get-tuple-element.8) | copy-start | bytes 1348

commit v3 on v2

--- a/solution.py
+++ b/solution.py
@@ -351,7 +351,7 @@
     dma = pltpu.SemaphoreType.DMA
     profiles, alignment = pl.pallas_call(
         functools.partial(body, blks, grps, rows),
-        out_shape=(jax.ShapeDtypeStruct((2, rows), jnp.float32), jax.ShapeDtypeStruct((1, 1), jnp.float32)),
+        out_shape=(pltpu.VMEM((2, rows), jnp.float32), pltpu.VMEM((1, 1), jnp.float32)),
         in_specs=[pl.BlockSpec(memory_space=pl.ANY), pl.BlockSpec(memory_space=pl.ANY), pl.BlockSpec(memory_space=pltpu.SMEM)],
         out_specs=(pl.BlockSpec(memory_space=pltpu.VMEM), pl.BlockSpec(memory_space=pltpu.VMEM)),
         scratch_shapes=[

time: 32.2 us -> 30.3 us (0.941)
  local copies, waits for them, and re-layouts: 1.21 us -> 0.56 us
  between operations: 2.41 us -> 1.8 us
  Pallas kernels: 28.4 us -> 27.8 us
    unnamed x3 -> x1, local copies, waits for them, and re-layouts: 1.21 us -> 0.56 us
    pallas_call x1, Pallas kernels: 28.4 us -> 27.8 us  [shards(): pl.pallas_call(functools.partial(body, blks, grps, rows), out_shape=(pltp...]
where the time goes in v3:
time: 30.3 us; the launch traced here: 30.2 us
  Pallas kernels  27.8 us (92%)
  between operations  1.8 us (6%)
  local copies, waits for them, and re-layouts  0.56 us (2%)
    pallas_call x1, Pallas kernels, shards(): pl.pallas_call(functools.partial(body, blks, grps, rows), out_shape=(pltp...  27.8 us

profile of v3, /device:TPU:0, one launch (start us, length us, event | category | flops | bytes accessed | tf_op | source)
XLA Modules:
  0.0 30.2 jit_solution(7436848395700468370)
XLA Ops:
  0.6 27.8 %shard_map.50 = (f32[2,56]{1,0:T(2,128)S(1)}, f32[1,1]{1,0:T(1,128)S(1)}) custom-call(bf16[56,1024]{1,0:T(8,128)(2,1)} %one_ref.1, bf16[56,1024]{1,0:T(8,128)(2,1)} %two_ref.1, s32[2]{0:T(128)} %spread_ref.1), custom_call_target="tpu_custom_call" | custom-call | tf_op jit(solution)/shard_map/pallas_call | solution.py:352
  28.5 0.6 %copy.7 = f32[2,56]{1,0:T(2,128)} copy(f32[2,56]{1,0:T(2,128)S(1)} %get-tuple-element.6) | data formatting | bytes 896
